TPU v7x, 32 devices: a whole 2x2x4 slice. The times are simulated.
32 devices in a mesh: dp: 8 (over z, x), section: 4 (over y, core).
Axes of the slice: x: 2, y: 2, z: 4, core: 2. Of those that a mesh axis runs over, the one named last changes fastest.
Arguments:
- entry_tokens: bfloat16 [8, 8, 16, 8192], P('dp'), may hold values from -6 to 6
- section_norm_gain: bfloat16 [4, 8192], P('section'), may hold values from 0.5 to 1.5
- adapter_down_weight: bfloat16 [4, 48, 8192], P('section'), may hold values from -0.0625 to 0.0625
- adapter_up_weight: bfloat16 [4, 48, 8192], P('section'), may hold values from -0.875 to 0.875
- output_gradient: bfloat16 [8, 8, 16, 8192], P('dp'), may hold values from -6 to 6
- lengths: int32 [8, 8], P('dp'), may hold values from 1 to 16
- keep: int32 [8, 4, 8, 16], P('dp', 'section'), may hold values from 0 to 1, as said below
Outputs:
- grad_up: float32 [4, 48, 8192], P('section')
- grad_gain: float32 [4, 8192], P('section')
Inputs may be any that keep to these rules, and one draw needn't show every extreme that they name: `keep`: 0 or 1; token 0 of every microbatch is kept at every section.
All inputs are finite; a program needn't handle non-finite values.
Results may differ from a plain program's by a relative error of at most 0.02.
Values may be sent and summed in bfloat16 or wider, within the bound.
A program may use at most 64 MiB of HBM per device.

v0:
```python
import functools

import jax
import jax.numpy as jnp
from jax import lax
from jax.experimental import pallas as pl
from jax.experimental.pallas import tpu as pltpu
from jax.sharding import PartitionSpec as P

EPS = 1e-05
NT = (((1,), (1,)), ((), ()))
TN = (((0,), (0,)), ((), ()))
MESH = pl.DeviceIdType.MESH
NN = (((1,), (0,)), ((), ()))


def mm(a, b, dims=NN, precision=None):
    return lax.dot_general(a, b, dims, precision=precision, preferred_element_type=jnp.float32)


def solve(au, uu, own, kept, valid, member, width, my):
    total, (rank, _) = len(au), au[0].shape
    rows = own[0].shape[1]
    bf = jnp.bfloat16
    norm2 = own[0][3 * rank:3 * rank + 1]
    r_now = jnp.concatenate([own[s][rank:2 * rank] for s in range(total)], axis=0)
    acc = jnp.concatenate([own[s][2 * rank:3 * rank] for s in range(total)], axis=0)
    zero = jnp.zeros((rank, rows), bf)
    cs, ps, invs, rs = [], [], [], []
    energy = jnp.zeros((1, rows), jnp.float32)
    count = jnp.zeros((1, rows), jnp.float32)
    for s in range(total):
        inv = lax.rsqrt(norm2 * (1.0 / width) + EPS)
        p = own[s][:rank]
        if s:
            p = p + mm(au[s], jnp.concatenate(cs + [zero] * (total - s), axis=0))
        c = (kept[s] * (p * inv).astype(bf).astype(jnp.float32)).astype(bf)
        cf = c.astype(jnp.float32)
        g = mm(uu[s], c, TN)
        quad = jnp.sum(cf * g[s * rank:(s + 1) * rank], axis=0, keepdims=True)
        cross = jnp.sum(cf * r_now[s * rank:(s + 1) * rank], axis=0, keepdims=True)
        rs.append(r_now)
        energy = energy + quad
        count = count + kept[s]
        norm2 = norm2 + 2.0 * cross + quad
        r_now = r_now + g
        cs.append(c)
        ps.append(p)
        invs.append(inv)
    sums = jnp.concatenate([energy, count, jnp.zeros((6, rows), jnp.float32)], axis=0)
    sums = mm(mm(sums, member, NT, lax.Precision.HIGHEST), member, NN, lax.Precision.HIGHEST)
    energy, count = sums[0:1], sums[1:2]
    scale = valid / (count * jnp.sqrt(energy / (width * count) + EPS))
    acc = acc * scale
    lams, alphas = [None] * total, [None] * total
    for s in reversed(range(total)):
        lam = (kept[s] * acc[s * rank:(s + 1) * rank]).astype(bf)
        lf = lam.astype(jnp.float32)
        alpha = invs[s] * invs[s] * invs[s] * jnp.sum(lf * ps[s], axis=0, keepdims=True) * (1.0 / width)
        lams[s] = (lf * invs[s]).astype(bf)
        alphas[s] = alpha
        if s:
            acc = acc + invs[s] * mm(au[s], lam, TN) - alpha * rs[s]
    c_all = jnp.concatenate(cs, axis=0)
    lam_all = jnp.concatenate(lams, axis=0)
    fl = lambda cond: jnp.where(cond, 1.0, 0.0).astype(jnp.float32)
    c_my = sum(fl(my == s) * cs[s].astype(jnp.float32) for s in range(total)).astype(bf)
    lam_my = sum(fl(my == s) * lams[s].astype(jnp.float32) for s in range(total)).astype(bf)
    beta = sum(fl(j > my) * alphas[j] for j in range(total))
    scaled_c = []
    for i in range(total):
        b = jnp.zeros((1, rows), jnp.float32)
        for j in range(i + 1, total):
            b = b + fl(j > my) * alphas[j]
        scaled_c.append((cs[i].astype(jnp.float32) * b).astype(bf))
    col = lax.broadcasted_iota(jnp.int32, (rank, total * rank), 1)
    mix = jnp.where(col < my * rank, mm(lam_my, c_all, NT),
                    jnp.where(col >= (my + 1) * rank, mm(c_my, lam_all, NT), 0.0))
    v = -mm(c_my, jnp.concatenate(scaled_c, axis=0), NT)
    m1 = (c_my.astype(jnp.float32) * scale).astype(bf)
    m2 = (-c_my.astype(jnp.float32) * beta).astype(bf)
    return m1, m2, lam_my, mix, v


def kernel(sizes, len_ref, keep_ref, gain_ref, e_hbm, g_hbm, d_hbm, u_hbm, out_ref, gout_ref,
           e_ref, g_ref, d_ref, u_ref, first_d, head, every, own_all, gram_tx, gram_rx, gram_all,
           tx, ttx, xrx, txrx, ztx, tztx, zrx, tzrx, mix_tx, mix_xrx, mix_ztx, mix_zrx, arx, tarx,
           load_sem, s1, r1, f1, s2, r2, s3, r3, s4, r4, sx, rx, stx, rtx, sz, rz, stz, rtz,
           smx, rmx, smz, rmz, sa, ra, sta, rta, sf, rf, stf, rtf):
    total, groups, inner, rank, micro, tok, width, part, model = sizes
    rows = micro * tok
    outer = groups // inner
    chunks = width // part
    tiles = part // 128
    bf, f32 = jnp.bfloat16, jnp.float32
    my = lax.axis_index("section")
    me = lax.axis_index("dp")
    z = me // inner
    x = me % inner

    def lanes(c):
        return pl.ds(pl.multiple_of(c * part, part), part)

    def ranks(s):
        return pl.ds(pl.multiple_of(s * rank, rank), rank)

    mine = jnp.minimum(me, chunks - 1)
    loads = [pltpu.make_async_copy(a, b, load_sem.at[i]) for i, (a, b) in enumerate(
        [(d_hbm.at[:, lanes(mine)], first_d), (u_hbm.at[:, lanes(mine)], head.at[1]),
         (e_hbm, e_ref), (d_hbm, d_ref), (u_hbm, u_ref), (g_hbm, g_ref)])]
    for load in loads:
        load.start()

    barrier = pltpu.get_barrier_semaphore()

    def greet_section(k, c):
        pl.semaphore_signal(barrier, inc=1, device_id={"section": (my + k) % total}, device_id_type=MESH)
        return c

    def greet_dp(k, c):
        pl.semaphore_signal(barrier, inc=1, device_id={"dp": (me + k) % groups}, device_id_type=MESH)
        return c

    lax.fori_loop(1, total, greet_section, 0)
    lax.fori_loop(1, groups, greet_dp, 0)

    def remote(src, dst, send, recv, **where):
        return pltpu.make_async_remote_copy(src_ref=src, dst_ref=dst, send_sem=send, recv_sem=recv,
                                            device_id=where, device_id_type=MESH)

    loads[0].wait()
    loads[1].wait()
    head[0] = (first_d[...].astype(f32) * gain_ref[:, lanes(mine)].astype(f32)).astype(bf)
    if chunks < groups:
        real = jnp.where(me < chunks, 1.0, 0.0).astype(f32)
        for i in range(2):
            head[i] = (head[i].astype(f32) * real).astype(bf)
    every[:, ranks(my), :] = head[...]

    lane = lax.broadcasted_iota(jnp.int32, (1, rows), 1)
    valid = jnp.zeros((1, rows), f32)
    for m in range(micro):
        valid = valid + jnp.where((lane >= m * tok) & (lane < m * tok + len_ref[0, m]), 1.0, 0.0)
    row8 = lax.broadcasted_iota(jnp.int32, (micro, rows), 0) * tok
    lane8 = lax.broadcasted_iota(jnp.int32, (micro, rows), 1)
    member = jnp.where((lane8 >= row8) & (lane8 < row8 + tok), 1.0, 0.0).astype(f32)
    row16 = lax.broadcasted_iota(jnp.int32, (tok, rows), 0)
    lane16 = lax.broadcasted_iota(jnp.int32, (tok, rows), 1)
    spread = jnp.zeros((tok, rows), f32)
    for m in range(micro):
        spread = spread + jnp.where(lane16 == row16 + m * tok, 1.0, 0.0)
    kept_row = valid * jnp.sum(mm(keep_ref[...].astype(f32), spread) * member, axis=0, keepdims=True)

    pl.semaphore_wait(barrier, total + groups - 2)

    step = 2 if total % 2 == 0 else 1
    mate = my + 1 - 2 * (my % 2)

    def weights(j, src):
        return remote(head, every.at[:, ranks(src), :], s1.at[j], r1.at[src], section=j)

    def share(src):
        return remote(every.at[:, ranks(src), :], every.at[:, ranks(src), :], f1.at[src], r1.at[src], section=mate)

    for k in range(step, total, step):
        weights((my + k) % total, my).start()
    if step == 2:
        weights(mate, my).start()

    loads[2].wait()
    loads[3].wait()
    loads[4].wait()

    def entry_chunk(c, acc):
        e = e_ref[:, lanes(c)]
        a = (d_ref[:, lanes(c)].astype(f32) * gain_ref[:, lanes(c)].astype(f32)).astype(bf)
        return (acc[0] + mm(jnp.concatenate([a, u_ref[:, lanes(c)]], axis=0), e, NT),
                acc[1] + mm(jnp.ones((8, part), bf), e * e, NT))

    zero = jnp.zeros((rank, rows), f32)
    sums = (jnp.zeros((2 * rank, rows), f32), jnp.zeros((8, rows), f32))
    sums = lax.fori_loop(0, chunks // 2, entry_chunk, sums)

    for k in range(step, total, step):
        src = (my + k) % total
        weights(my, src).wait_recv()
        if step == 2:
            share(src).start()

    def owns(j, src):
        return remote(own_all.at[src], own_all.at[src], s2.at[j], r2.at[src], section=j)

    if step == 2:
        for k in range(0, total, 2):
            weights(my, (mate + k) % total).wait_recv()
    gram_tx[...] = jnp.concatenate([mm(head[0], every[1], NT), mm(head[1], every[1], NT)], axis=0).astype(bf)

    def grams(j, src):
        return remote(gram_tx, gram_rx.at[src], s3.at[j], r3.at[src], dp=j)

    def send_gram(k, c):
        grams((me + k) % groups, me).start()
        return c

    lax.fori_loop(1, groups, send_gram, 0)

    aue, nn = lax.fori_loop(chunks // 2, chunks, entry_chunk, sums)
    loads[5].wait()
    ug = lax.fori_loop(0, chunks, lambda c, acc: acc + mm(u_ref[:, lanes(c)], g_ref[:, lanes(c)], NT), zero)
    own_all[my] = jnp.concatenate([aue, ug, nn, jnp.broadcast_to(kept_row, (8, rows))], axis=0)
    for k in range(1, total):
        owns((my + k) % total, my).start()

    gram_rx[me] = gram_tx[...]

    def wait_gram(k, c):
        grams(me, (me + k) % groups).wait_recv()
        return c

    lax.fori_loop(1, groups, wait_gram, 0)
    gram = lax.fori_loop(0, groups, lambda k, acc: acc + gram_rx[k].astype(f32),
                         jnp.zeros((2 * rank, total * rank), f32))
    gram_all[my] = gram.astype(bf)

    def all_grams(j, src):
        return remote(gram_all.at[src], gram_all.at[src], s4.at[j], r4.at[src], section=j)

    for k in range(1, total):
        all_grams((my + k) % total, my).start()
    for k in range(1, total):
        owns(my, (my + k) % total).wait_recv()
    for k in range(1, total):
        all_grams(my, (my + k) % total).wait_recv()

    au = [gram_all[s, :rank] for s in range(total)]
    uu = [gram_all[s, rank:] for s in range(total)]
    own = [own_all[s] for s in range(total)]
    kept = [own_all[s, 3 * rank + 8:3 * rank + 9] for s in range(total)]
    m1, m2, lam, mix, v = solve(au, uu, own, kept, valid, member, model, my)

    left = jnp.concatenate([jnp.concatenate([m1, m2], axis=1),
                            jnp.concatenate([jnp.zeros_like(lam), lam], axis=1)], axis=0)

    peer = me + 1 - 2 * x
    mix_tx[0] = mix.astype(bf)
    mix_tx[1] = v.astype(bf)

    def mix_x():
        return remote(mix_tx, mix_xrx, smx, rmx, dp=peer)

    def mix_z(j, src):
        return remote(mix_ztx, mix_zrx.at[src], smz.at[j], rmz.at[src], dp=j * inner + x)

    def piece(c):
        e = e_ref[:, lanes(c)]
        both = mm(left, jnp.concatenate([g_ref[:, lanes(c)], e], axis=0))
        row = jnp.sum(d_ref[:, lanes(c)].astype(f32) * both[rank:], axis=0, keepdims=True)
        return both[:rank], row

    def put_row(ref, row):
        for i in range(tiles):
            ref[i:i + 1, :] = row[:, 128 * i:128 * (i + 1)]

    def send_x(q):
        return (remote(tx.at[q], xrx.at[q], sx.at[q], rx.at[q], dp=peer),
                remote(ttx.at[q], txrx.at[q], stx.at[q], rtx.at[q], dp=peer))

    def send_z(q, src):
        return (remote(ztx.at[q], zrx.at[src], sz.at[q], rz.at[src], dp=q * inner + x),
                remote(tztx.at[q], tzrx.at[src], stz.at[q], rtz.at[src], dp=q * inner + x))

    if inner > 1:
        mix_x().start()

        def first(k, carry):
            q = (z + 1 + k) % outer
            c = q * inner + 1 - x
            big, row = piece(jnp.minimum(c, chunks - 1))
            tx[q] = big.astype(bf)
            put_row(ttx.at[q], row)
            for copy in send_x(q):
                copy.start()
            return carry

        lax.fori_loop(0, outer, first, 0)
        mix_x().wait_recv()
        for i in range(2):
            mix_ztx[i] = (mix_tx[i].astype(f32) + mix_xrx[i].astype(f32)).astype(bf)
    else:
        mix_ztx[...] = mix_tx[...]
    for k in range(1, outer):
        mix_z((z + k) % outer, z).start()

    def second(k, carry):
        q = (z + 1 + k) % outer
        big, row = piece(jnp.minimum(q * inner + x, chunks - 1))
        put_row(tztx.at[q], row)
        if inner > 1:
            for copy in send_x(q):
                copy.wait_recv()
            big = big + xrx[q].astype(f32)
            tztx[q, :tiles] = tztx[q, :tiles] + txrx[q, :tiles]
        ztx[q] = big.astype(bf)

        @pl.when(k < outer - 1)
        def _():
            for copy in send_z(q, z):
                copy.start()
        return carry

    lax.fori_loop(0, outer, second, 0)

    mixed = [mix_ztx[i].astype(f32) for i in range(2)]
    for k in range(1, outer):
        q = (z + k) % outer
        mix_z(z, q).wait_recv()
        mixed = [mixed[i] + mix_zrx[q, i].astype(f32) for i in range(2)]
    col = lax.broadcasted_iota(jnp.int32, (rank, total * rank), 1)
    low = jnp.where(col < my * rank, mixed[0], 0.0).astype(bf)
    high = jnp.where(col < my * rank, 0.0, mixed[0]).astype(bf)
    big = mm(high, every[0]) + mm(mixed[1].astype(bf), every[1]) + ztx[z].astype(f32)
    row = jnp.sum(d_ref[:, lanes(mine)].astype(f32) * mm(low, every[1]), axis=0, keepdims=True)
    put_row(tarx.at[me], row)
    tall = tarx[me, :tiles] + tztx[z, :tiles]
    for k in range(1, outer):
        q = (z + k) % outer
        for copy in send_z(z, q):
            copy.wait_recv()
        big = big + zrx[q].astype(f32)
        tall = tall + tzrx[q, :tiles]
    tarx[me, :tiles] = tall
    arx[me] = big.astype(bf)

    def gather_z(j, src):
        c = src * inner + x
        return (remote(arx.at[c], arx.at[c], sa.at[j], ra.at[src], dp=j * inner + x),
                remote(tarx.at[c], tarx.at[c], sta.at[j], rta.at[src], dp=j * inner + x))

    def gather_x(q, side):
        c = q * inner + side
        return (remote(arx.at[c], arx.at[c], sf.at[q], rf.at[q], dp=peer),
                remote(tarx.at[c], tarx.at[c], stf.at[q], rtf.at[q], dp=peer))

    def write(c):
        def go():
            out_ref[:, lanes(c)] = arx[c].astype(f32)
            for i in range(tiles):
                gout_ref[:, pl.ds(pl.multiple_of(c * part + 128 * i, 128), 128)] = tarx[c, i:i + 1, :]
        if chunks == groups:
            go()
        else:
            pl.when(c < chunks)(go)

    for k in range(1, outer):
        for copy in gather_z((z + k) % outer, z):
            copy.start()
    if inner > 1:
        for copy in gather_x(z, x):
            copy.start()
    write(me)

    def pass_on(k, carry):
        q = (z + k) % outer
        for copy in gather_z(z, q):
            copy.wait_recv()
        if inner > 1:
            for copy in gather_x(q, x):
                copy.start()
        write(q * inner + x)
        return carry

    lax.fori_loop(1, outer, pass_on, 0)

    if inner > 1:
        def last(k, carry):
            q = (z + k) % outer
            for copy in gather_x(q, 1 - x):
                copy.wait_recv()
            write(q * inner + 1 - x)
            return carry

        lax.fori_loop(0, outer, last, 0)

    for k in range(step, total, step):
        weights((my + k) % total, my).wait_send()
        if step == 2:
            share((my + k) % total).wait_send()
    if step == 2:
        weights(mate, my).wait_send()
    for k in range(1, total):
        j = (my + k) % total
        owns(j, my).wait_send()
        all_grams(j, my).wait_send()

    def left_dp(k, carry):
        grams((me + k) % groups, me).wait_send()
        return carry

    lax.fori_loop(1, groups, left_dp, 0)

    def left_z(k, carry):
        q = (z + k) % outer
        mix_z(q, z).wait_send()
        for copy in send_z(q, z) + gather_z(q, z):
            copy.wait_send()
        return carry

    lax.fori_loop(1, outer, left_z, 0)
    if inner > 1:
        mix_x().wait_send()

        def left_x(q, carry):
            for copy in send_x(q) + gather_x(q, x):
                copy.wait_send()
            return carry

        lax.fori_loop(0, outer, left_x, 0)


def body(entry, gain, down, up, gout, lengths, keep):
    bf, f32 = jnp.bfloat16, jnp.float32
    total = lax.axis_size("section")
    groups = lax.axis_size("dp")
    micro, tok, width = entry.shape[1:]
    rank = down.shape[1]
    rows = micro * tok
    part = 128 * (-(-width // (128 * groups)))
    pad = -width % part
    wide = width + pad
    inner = 2 if groups % 2 == 0 else 1
    outer = groups // inner
    widen = lambda a: jnp.pad(a, ((0, 0), (0, pad))) if pad else a
    e = widen(entry[0].reshape(rows, width))
    go = widen(gout[0].reshape(rows, width))
    d, u = widen(down[0]), widen(up[0])
    tall = max(8, part // 128)
    sizes = (total, groups, inner, rank, micro, tok, wide, part, width)
    vm = lambda *s, t=bf: pltpu.VMEM(s, t)
    dma = lambda *n: pltpu.SemaphoreType.DMA(n)
    scratch = [
        vm(rows, wide), vm(rows, wide), vm(rank, wide), vm(rank, wide),
        vm(rank, part), vm(2, rank, part), vm(2, total * rank, part),
        vm(total, 3 * rank + 16, rows, t=f32),
        vm(2 * rank, total * rank), vm(groups, 2 * rank, total * rank), vm(total, 2 * rank, total * rank),
        vm(outer, rank, part), vm(outer, tall, 128, t=f32), vm(outer, rank, part), vm(outer, tall, 128, t=f32),
        vm(outer, rank, part), vm(outer, tall, 128, t=f32), vm(outer, rank, part), vm(outer, tall, 128, t=f32),
        vm(2, rank, total * rank), vm(2, rank, total * rank), vm(2, rank, total * rank),
        vm(outer, 2, rank, total * rank),
        vm(groups, rank, part), vm(groups, tall, 128, t=f32),
        dma(6), dma(total), dma(total), dma(total), dma(total), dma(total), dma(groups), dma(groups), dma(total), dma(total),
        dma(outer), dma(outer), dma(outer), dma(outer), dma(outer), dma(outer), dma(outer), dma(outer),
        pltpu.SemaphoreType.DMA, pltpu.SemaphoreType.DMA, dma(outer), dma(outer),
        dma(outer), dma(outer), dma(outer), dma(outer), dma(outer), dma(outer), dma(outer), dma(outer),
    ]
    inside = pl.BlockSpec(memory_space=pltpu.VMEM)
    outside = pl.BlockSpec(memory_space=pl.ANY)
    up_grad, gain_grad = pl.pallas_call(
        functools.partial(kernel, sizes),
        out_shape=(jax.ShapeDtypeStruct((rank, wide), f32), jax.ShapeDtypeStruct((1, wide), f32)),
        in_specs=[pl.BlockSpec(memory_space=pltpu.SMEM)] + [inside] * 2 + [outside] * 4,
        out_specs=(inside, inside),
        scratch_shapes=scratch,
        compiler_params=pltpu.CompilerParams(
            collective_id=0, has_side_effects=True, vmem_limit_bytes=60 * 1024 * 1024),
        name="relay",
    )(lengths, keep[0, 0], widen(gain), e, go, d, u)
    return up_grad[None, :, :width], gain_grad[:, :width]


def solution(mesh):
    in_specs = (
        P("dp", None, None, None),
        P("section", None),
        P("section", None, None),
        P("section", None, None),
        P("dp", None, None, None),
        P("dp", None),
        P("dp", "section", None, None),
    )
    out_specs = (P("section", None, None), P("section", None))
    return jax.shard_map(body, mesh=mesh, in_specs=in_specs, out_specs=out_specs, check_vma=False)
```

profile of v0, /device:TPU:0, one launch (start us, length us, event | category | flops | bytes accessed | tf_op | source)
XLA Modules:
  0.0 66.4 jit_solution(14274584232328160770)
XLA Ops:
  0.6 62.5 %relay.1 = (f32[48,8192]{1,0:T(8,128)}, f32[1,8192]{1,0:T(1,128)}) custom-call(s32[1,8]{1,0:T(1,128)} %len_ref.1, s32[8,16]{1,0:T(8,128)} %bitcast.11, bf16[1,8192]{1,0:T(2,128)(2,1)} %gain_ref.1, bf16[128,8192]{1,0:T(8,128)(2,1)} %bitcast.6, bf16[128,8192]{1,0:T(8,128)(2,1)} %bitcast.7, bf16[48,8192]{1,0:T(8,128)(2,1)} %bitcast.9, bf16[48,8192]{1,0:T(8,128)(2,1)} %bitcast.10), custom_call_target="tpu_custom_call" | custom-call | tf_op jit(solution)/shard_map/relay/pallas_call | solution.py:457
  63.1 0.0 copy-start
  63.1 2.7 %copy.11 = f32[1,48,8192]{2,1,0:T(8,128)} copy(f32[1,48,8192]{2,1,0:T(8,128)} %bitcast.8) | data formatting | bytes 3145728
  65.8 0.0 copy-done
  65.8 0.6 copy.12
Async XLA Ops:
  63.1 2.7 %copy-start = (f32[1,8192]{1,0:T(1,128)S(1)}, f32[1,8192]{1,0:T(1,128)}, u32[]{:S(2)}) copy-start(f32[1,8192]{1,0:T(1,128)} %get-tuple-element.9) | copy-start | bytes 98308
where the time goes:
time: 66.6 us; the launch traced here: 66.4 us
  Pallas kernels  62.5 us (94%)
  local copies, waits for them, and re-layouts  3.28 us (5%)
    pallas_call x1, Pallas kernels, body(): pl.pallas_call(functools.partial(kernel, sizes), out_shape=(jax.ShapeDtyp...  62.5 us
    unnamed x4, local copies, waits for them, and re-layouts  3.28 us

commit v1 on v0

--- a/solution.py
+++ b/solution.py
@@ -82,8 +82,8 @@
     return m1, m2, lam_my, mix, v
 
 
-def kernel(sizes, len_ref, keep_ref, gain_ref, e_hbm, g_hbm, d_hbm, u_hbm, out_ref, gout_ref,
-           e_ref, g_ref, d_ref, u_ref, first_d, head, every, own_all, gram_tx, gram_rx, gram_all,
+def kernel(sizes, len_hbm, keep_hbm, gain_hbm, e_hbm, g_hbm, d_hbm, u_hbm, out_ref, gout_ref,
+           len_ref, keep_ref, gain_ref, e_ref, g_ref, d_ref, u_ref, first_d, head, every, own_all, gram_tx, gram_rx, gram_all,
            tx, ttx, xrx, txrx, ztx, tztx, zrx, tzrx, mix_tx, mix_xrx, mix_ztx, mix_zrx, arx, tarx,
            load_sem, s1, r1, f1, s2, r2, s3, r3, s4, r4, sx, rx, stx, rtx, sz, rz, stz, rtz,
            smx, rmx, smz, rmz, sa, ra, sta, rta, sf, rf, stf, rtf):
@@ -107,7 +107,8 @@
     mine = jnp.minimum(me, chunks - 1)
     loads = [pltpu.make_async_copy(a, b, load_sem.at[i]) for i, (a, b) in enumerate(
         [(d_hbm.at[:, lanes(mine)], first_d), (u_hbm.at[:, lanes(mine)], head.at[1]),
-         (e_hbm, e_ref), (d_hbm, d_ref), (u_hbm, u_ref), (g_hbm, g_ref)])]
+         (e_hbm, e_ref), (d_hbm, d_ref), (u_hbm, u_ref), (g_hbm, g_ref),
+         (gain_hbm, gain_ref), (keep_hbm, keep_ref), (len_hbm, len_ref)])]
     for load in loads:
         load.start()
 
@@ -128,8 +129,8 @@
         return pltpu.make_async_remote_copy(src_ref=src, dst_ref=dst, send_sem=send, recv_sem=recv,
                                             device_id=where, device_id_type=MESH)
 
-    loads[0].wait()
-    loads[1].wait()
+    for i in (0, 1, 6, 7, 8):
+        loads[i].wait()
     head[0] = (first_d[...].astype(f32) * gain_ref[:, lanes(mine)].astype(f32)).astype(bf)
     if chunks < groups:
         real = jnp.where(me < chunks, 1.0, 0.0).astype(f32)
@@ -343,7 +344,7 @@
 
     def write(c):
         def go():
-            out_ref[:, lanes(c)] = arx[c].astype(f32)
+            out_ref[:, lanes(c)] = arx[c]
             for i in range(tiles):
                 gout_ref[:, pl.ds(pl.multiple_of(c * part + 128 * i, 128), 128)] = tarx[c, i:i + 1, :]
         if chunks == groups:
@@ -430,14 +431,16 @@
     inner = 2 if groups % 2 == 0 else 1
     outer = groups // inner
     widen = lambda a: jnp.pad(a, ((0, 0), (0, pad))) if pad else a
-    e = widen(entry[0].reshape(rows, width))
-    go = widen(gout[0].reshape(rows, width))
-    d, u = widen(down[0]), widen(up[0])
+    hold = lambda a: pltpu.with_memory_space_constraint(a, pltpu.HBM)
+    e = hold(widen(entry[0].reshape(rows, width)))
+    go = hold(widen(gout[0].reshape(rows, width)))
+    d, u = hold(widen(down[0])), hold(widen(up[0]))
     tall = max(8, part // 128)
     sizes = (total, groups, inner, rank, micro, tok, wide, part, width)
     vm = lambda *s, t=bf: pltpu.VMEM(s, t)
     dma = lambda *n: pltpu.SemaphoreType.DMA(n)
     scratch = [
+        pltpu.SMEM((1, micro), jnp.int32), vm(micro, tok, t=jnp.int32), vm(1, wide),
         vm(rows, wide), vm(rows, wide), vm(rank, wide), vm(rank, wide),
         vm(rank, part), vm(2, rank, part), vm(2, total * rank, part),
         vm(total, 3 * rank + 16, rows, t=f32),
@@ -447,24 +450,24 @@
         vm(2, rank, total * rank), vm(2, rank, total * rank), vm(2, rank, total * rank),
         vm(outer, 2, rank, total * rank),
         vm(groups, rank, part), vm(groups, tall, 128, t=f32),
-        dma(6), dma(total), dma(total), dma(total), dma(total), dma(total), dma(groups), dma(groups), dma(total), dma(total),
+        dma(9), dma(total), dma(total), dma(total), dma(total), dma(total), dma(groups), dma(groups), dma(total), dma(total),
         dma(outer), dma(outer), dma(outer), dma(outer), dma(outer), dma(outer), dma(outer), dma(outer),
         pltpu.SemaphoreType.DMA, pltpu.SemaphoreType.DMA, dma(outer), dma(outer),
         dma(outer), dma(outer), dma(outer), dma(outer), dma(outer), dma(outer), dma(outer), dma(outer),
     ]
     inside = pl.BlockSpec(memory_space=pltpu.VMEM)
-    outside = pl.BlockSpec(memory_space=pl.ANY)
+    outside = pl.BlockSpec(memory_space=pltpu.HBM)
     up_grad, gain_grad = pl.pallas_call(
         functools.partial(kernel, sizes),
-        out_shape=(jax.ShapeDtypeStruct((rank, wide), f32), jax.ShapeDtypeStruct((1, wide), f32)),
-        in_specs=[pl.BlockSpec(memory_space=pltpu.SMEM)] + [inside] * 2 + [outside] * 4,
+        out_shape=(jax.ShapeDtypeStruct((rank, wide), bf), jax.ShapeDtypeStruct((1, wide), f32)),
+        in_specs=[outside] * 7,
         out_specs=(inside, inside),
         scratch_shapes=scratch,
         compiler_params=pltpu.CompilerParams(
-            collective_id=0, has_side_effects=True, vmem_limit_bytes=60 * 1024 * 1024),
+            collective_id=0, has_side_effects=True, vmem_limit_bytes=48 * 1024 * 1024),
         name="relay",
-    )(lengths, keep[0, 0], widen(gain), e, go, d, u)
-    return up_grad[None, :, :width], gain_grad[:, :width]
+    )(hold(lengths), hold(keep[0, 0]), hold(widen(gain)), e, go, d, u)
+    return up_grad[None, :, :width].astype(f32), gain_grad[:, :width]
 
 
 def solution(mesh):

time: 66.6 us -> 64 us (0.961)
  local copies, waits for them, and re-layouts: 3.28 us -> 0.61 us
  other arithmetic: 0 us -> 1.25 us
  Pallas kernels: 62.5 us -> 61.3 us
    unnamed x4 -> x1, local copies, waits for them, and re-layouts: 3.28 us -> 0.61 us
    convert_element_type x0 -> x1, other arithmetic: none -> 1.25 us  [body(): return (up_grad[None, :, :width].astype(f32), gain_grad[:, :width])]
    pallas_call x1, Pallas kernels: 62.5 us -> 61.3 us  [body(): pl.pallas_call(functools.partial(kernel, sizes), out_shape=(jax.ShapeDtyp...]
where the time goes in v1:
time: 64 us; the launch traced here: 63.8 us
  Pallas kernels  61.3 us (96%)
  other arithmetic  1.25 us (2%)
  between operations  0.64 us (1%)
    pallas_call x1, Pallas kernels, body(): pl.pallas_call(functools.partial(kernel, sizes), out_shape=(jax.ShapeDtyp...  61.3 us

profile of v1, /device:TPU:0, one launch (start us, length us, event | category | flops | bytes accessed | tf_op | source)
XLA Modules:
  0.0 63.8 jit_solution(8637811525266937027)
XLA Ops:
  0.6 61.3 %relay.1 = (bf16[48,8192]{1,0:T(8,128)(2,1)S(1)}, f32[1,8192]{1,0:T(1,128)S(1)}) custom-call(s32[1,8]{1,0:T(1,128)} %len_hbm.1, s32[8,16]{1,0:T(8,128)} %bitcast.12, bf16[1,8192]{1,0:T(2,128)(2,1)} %gain_hbm.1, bf16[128,8192]{1,0:T(8,128)(2,1)} %bitcast.8, bf16[128,8192]{1,0:T(8,128)(2,1)} %bitcast.9, bf16[48,8192]{1,0:T(8,128)(2,1)} %bitcast.10, ...), custom_call_target="tpu_custom_call" | custom-call | tf_op jit(solution)/shard_map/relay/pallas_call | solution.py:460
  61.9 1.2 %bitcast_convert_fusion = f32[1,48,8192]{2,1,0:T(8,128)} fusion(bf16[48,8192]{1,0:T(8,128)(2,1)S(1)} %get-tuple-element.4), kind=kLoop, calls=%fused_computation | loop fusion | flops 393216 | bytes 2359296 | tf_op jit(solution)/shard_map/convert_element_type | solution.py:470
  63.2 0.6 copy.10

commit v2 on v1

--- a/solution.py
+++ b/solution.py
@@ -83,7 +83,7 @@
 
 
 def kernel(sizes, len_hbm, keep_hbm, gain_hbm, e_hbm, g_hbm, d_hbm, u_hbm, out_ref, gout_ref,
-           len_ref, keep_ref, gain_ref, e_ref, g_ref, d_ref, u_ref, first_d, head, every, own_all, gram_tx, gram_rx, gram_all,
+           len_ref, keep_ref, gain_ref, e_ref, g_ref, d_ref, u_ref, every, own_all, gram_tx, gram_rx, gram_all,
            tx, ttx, xrx, txrx, ztx, tztx, zrx, tzrx, mix_tx, mix_xrx, mix_ztx, mix_zrx, arx, tarx,
            load_sem, s1, r1, f1, s2, r2, s3, r3, s4, r4, sx, rx, stx, rtx, sz, rz, stz, rtz,
            smx, rmx, smz, rmz, sa, ra, sta, rta, sf, rf, stf, rtf):
@@ -106,9 +106,9 @@
 
     mine = jnp.minimum(me, chunks - 1)
     loads = [pltpu.make_async_copy(a, b, load_sem.at[i]) for i, (a, b) in enumerate(
-        [(d_hbm.at[:, lanes(mine)], first_d), (u_hbm.at[:, lanes(mine)], head.at[1]),
-         (e_hbm, e_ref), (d_hbm, d_ref), (u_hbm, u_ref), (g_hbm, g_ref),
-         (gain_hbm, gain_ref), (keep_hbm, keep_ref), (len_hbm, len_ref)])]
+        [(u_hbm.at[:, lanes(mine)], every.at[1, ranks(my), :]),
+         (gain_hbm, gain_ref), (keep_hbm, keep_ref), (len_hbm, len_ref),
+         (e_hbm, e_ref), (d_hbm, d_ref), (u_hbm, u_ref), (g_hbm, g_ref)])]
     for load in loads:
         load.start()
 
@@ -129,14 +129,11 @@
         return pltpu.make_async_remote_copy(src_ref=src, dst_ref=dst, send_sem=send, recv_sem=recv,
                                             device_id=where, device_id_type=MESH)
 
-    for i in (0, 1, 6, 7, 8):
+    for i in range(4):
         loads[i].wait()
-    head[0] = (first_d[...].astype(f32) * gain_ref[:, lanes(mine)].astype(f32)).astype(bf)
+    real = jnp.where(me < chunks, 1.0, 0.0).astype(f32)
     if chunks < groups:
-        real = jnp.where(me < chunks, 1.0, 0.0).astype(f32)
-        for i in range(2):
-            head[i] = (head[i].astype(f32) * real).astype(bf)
-    every[:, ranks(my), :] = head[...]
+        every[1, ranks(my), :] = (every[1, ranks(my), :].astype(f32) * real).astype(bf)
 
     lane = lax.broadcasted_iota(jnp.int32, (1, rows), 1)
     valid = jnp.zeros((1, rows), f32)
@@ -157,20 +154,36 @@
     step = 2 if total % 2 == 0 else 1
     mate = my + 1 - 2 * (my % 2)
 
-    def weights(j, src):
-        return remote(head, every.at[:, ranks(src), :], s1.at[j], r1.at[src], section=j)
-
-    def share(src):
-        return remote(every.at[:, ranks(src), :], every.at[:, ranks(src), :], f1.at[src], r1.at[src], section=mate)
-
-    for k in range(step, total, step):
-        weights((my + k) % total, my).start()
-    if step == 2:
-        weights(mate, my).start()
-
-    loads[2].wait()
-    loads[3].wait()
-    loads[4].wait()
+    def block(w, src):
+        return every.at[w, ranks(src), :]
+
+    def weights(w, j, src):
+        return remote(block(w, src), block(w, src), s1.at[w, j], r1.at[w, src], section=j)
+
+    def share(w, src):
+        return remote(block(w, src), block(w, src), f1.at[w, src], r1.at[w, src], section=mate)
+
+    def send_weights(w):
+        for k in range(step, total, step):
+            weights(w, (my + k) % total, my).start()
+        if step == 2:
+            weights(w, mate, my).start()
+
+    def pass_weights(w):
+        for k in range(step, total, step):
+            src = (my + k) % total
+            weights(w, my, src).wait_recv()
+            if step == 2:
+                share(w, src).start()
+
+    def wait_weights(w):
+        if step == 2:
+            for k in range(0, total, 2):
+                weights(w, my, (mate + k) % total).wait_recv()
+
+    send_weights(1)
+    for i in range(4, 7):
+        loads[i].wait()
 
     def entry_chunk(c, acc):
         e = e_ref[:, lanes(c)]
@@ -180,21 +193,26 @@
 
     zero = jnp.zeros((rank, rows), f32)
     sums = (jnp.zeros((2 * rank, rows), f32), jnp.zeros((8, rows), f32))
-    sums = lax.fori_loop(0, chunks // 2, entry_chunk, sums)
-
-    for k in range(step, total, step):
-        src = (my + k) % total
-        weights(my, src).wait_recv()
-        if step == 2:
-            share(src).start()
+    aue, nn = lax.fori_loop(0, chunks, entry_chunk, sums)
+    loads[7].wait()
+    ug = lax.fori_loop(0, chunks, lambda c, acc: acc + mm(u_ref[:, lanes(c)], g_ref[:, lanes(c)], NT), zero)
+    own_all[my] = jnp.concatenate([aue, ug, nn, jnp.broadcast_to(kept_row, (8, rows))], axis=0)
 
     def owns(j, src):
         return remote(own_all.at[src], own_all.at[src], s2.at[j], r2.at[src], section=j)
 
-    if step == 2:
-        for k in range(0, total, 2):
-            weights(my, (mate + k) % total).wait_recv()
-    gram_tx[...] = jnp.concatenate([mm(head[0], every[1], NT), mm(head[1], every[1], NT)], axis=0).astype(bf)
+    for k in range(1, total):
+        owns((my + k) % total, my).start()
+    every[0, ranks(my), :] = (d_ref[:, lanes(mine)].astype(f32) * gain_ref[:, lanes(mine)].astype(f32)
+                              * real).astype(bf)
+    send_weights(0)
+
+    pass_weights(1)
+    wait_weights(1)
+    size = total * rank
+    col = lax.broadcasted_iota(jnp.int32, (rank, size), 1)
+    both = mm(jnp.concatenate([every[0, ranks(my), :], every[1, ranks(my), :]], axis=0), every[1], NT)
+    gram_tx[...] = jnp.where(col < my * rank, both[:rank], both[rank:]).astype(bf)
 
     def grams(j, src):
         return remote(gram_tx, gram_rx.at[src], s3.at[j], r3.at[src], dp=j)
@@ -204,14 +222,7 @@
         return c
 
     lax.fori_loop(1, groups, send_gram, 0)
-
-    aue, nn = lax.fori_loop(chunks // 2, chunks, entry_chunk, sums)
-    loads[5].wait()
-    ug = lax.fori_loop(0, chunks, lambda c, acc: acc + mm(u_ref[:, lanes(c)], g_ref[:, lanes(c)], NT), zero)
-    own_all[my] = jnp.concatenate([aue, ug, nn, jnp.broadcast_to(kept_row, (8, rows))], axis=0)
-    for k in range(1, total):
-        owns((my + k) % total, my).start()
-
+    pass_weights(0)
     gram_rx[me] = gram_tx[...]
 
     def wait_gram(k, c):
@@ -219,12 +230,11 @@
         return c
 
     lax.fori_loop(1, groups, wait_gram, 0)
-    gram = lax.fori_loop(0, groups, lambda k, acc: acc + gram_rx[k].astype(f32),
-                         jnp.zeros((2 * rank, total * rank), f32))
-    gram_all[my] = gram.astype(bf)
+    gram = lax.fori_loop(0, groups, lambda k, acc: acc + gram_rx[k].astype(f32), jnp.zeros((rank, size), f32))
+    gram_all[ranks(my), :] = gram.astype(bf)
 
     def all_grams(j, src):
-        return remote(gram_all.at[src], gram_all.at[src], s4.at[j], r4.at[src], section=j)
+        return remote(gram_all.at[ranks(src), :], gram_all.at[ranks(src), :], s4.at[j], r4.at[src], section=j)
 
     for k in range(1, total):
         all_grams((my + k) % total, my).start()
@@ -233,8 +243,13 @@
     for k in range(1, total):
         all_grams(my, (my + k) % total).wait_recv()
 
-    au = [gram_all[s, :rank] for s in range(total)]
-    uu = [gram_all[s, rank:] for s in range(total)]
+    table = gram_all[...]
+    eye = jnp.where(lax.broadcasted_iota(jnp.int32, (size, size), 0)
+                    == lax.broadcasted_iota(jnp.int32, (size, size), 1), 1.0, 0.0).astype(bf)
+    turned = mm(table, eye, TN)
+    au = [table[s * rank:(s + 1) * rank] for s in range(total)]
+    uu = [jnp.where(col >= s * rank, au[s].astype(f32), turned[s * rank:(s + 1) * rank]).astype(bf)
+          for s in range(total)]
     own = [own_all[s] for s in range(total)]
     kept = [own_all[s, 3 * rank + 8:3 * rank + 9] for s in range(total)]
     m1, m2, lam, mix, v = solve(au, uu, own, kept, valid, member, model, my)
@@ -311,6 +326,7 @@
 
     lax.fori_loop(0, outer, second, 0)
 
+    wait_weights(0)
     mixed = [mix_ztx[i].astype(f32) for i in range(2)]
     for k in range(1, outer):
         q = (z + k) % outer
@@ -382,12 +398,13 @@
 
         lax.fori_loop(0, outer, last, 0)
 
-    for k in range(step, total, step):
-        weights((my + k) % total, my).wait_send()
+    for w in range(2):
+        for k in range(step, total, step):
+            weights(w, (my + k) % total, my).wait_send()
+            if step == 2:
+                share(w, (my + k) % total).wait_send()
         if step == 2:
-            share((my + k) % total).wait_send()
-    if step == 2:
-        weights(mate, my).wait_send()
+            weights(w, mate, my).wait_send()
     for k in range(1, total):
         j = (my + k) % total
         owns(j, my).wait_send()
@@ -442,15 +459,15 @@
     scratch = [
         pltpu.SMEM((1, micro), jnp.int32), vm(micro, tok, t=jnp.int32), vm(1, wide),
         vm(rows, wide), vm(rows, wide), vm(rank, wide), vm(rank, wide),
-        vm(rank, part), vm(2, rank, part), vm(2, total * rank, part),
+        vm(2, total * rank, part),
         vm(total, 3 * rank + 16, rows, t=f32),
-        vm(2 * rank, total * rank), vm(groups, 2 * rank, total * rank), vm(total, 2 * rank, total * rank),
+        vm(rank, total * rank), vm(groups, rank, total * rank), vm(total * rank, total * rank),
         vm(outer, rank, part), vm(outer, tall, 128, t=f32), vm(outer, rank, part), vm(outer, tall, 128, t=f32),
         vm(outer, rank, part), vm(outer, tall, 128, t=f32), vm(outer, rank, part), vm(outer, tall, 128, t=f32),
         vm(2, rank, total * rank), vm(2, rank, total * rank), vm(2, rank, total * rank),
         vm(outer, 2, rank, total * rank),
         vm(groups, rank, part), vm(groups, tall, 128, t=f32),
-        dma(9), dma(total), dma(total), dma(total), dma(total), dma(total), dma(groups), dma(groups), dma(total), dma(total),
+        dma(8), dma(2, total), dma(2, total), dma(2, total), dma(total), dma(total), dma(groups), dma(groups), dma(total), dma(total),
         dma(outer), dma(outer), dma(outer), dma(outer), dma(outer), dma(outer), dma(outer), dma(outer),
         pltpu.SemaphoreType.DMA, pltpu.SemaphoreType.DMA, dma(outer), dma(outer),
         dma(outer), dma(outer), dma(outer), dma(outer), dma(outer), dma(outer), dma(outer), dma(outer),

time: 64 us -> 57.4 us (0.90)
  Pallas kernels: 61.3 us -> 54.1 us
    pallas_call x1, Pallas kernels: 61.3 us -> 54.1 us  [body(): pl.pallas_call(functools.partial(kernel, sizes), out_shape=(jax.ShapeDtyp...]
where the time goes in v2:
time: 57.4 us; the launch traced here: 56.6 us
  Pallas kernels  54.1 us (94%)
  other arithmetic  1.25 us (2%)
  between operations  0.64 us (1%)
  local copies, waits for them, and re-layouts  0.61 us (1%)
    pallas_call x1, Pallas kernels, body(): pl.pallas_call(functools.partial(kernel, sizes), out_shape=(jax.ShapeDtyp...  54.1 us
    convert_element_type x1, other arithmetic, body(): return (up_grad[None, :, :width].astype(f32), gain_grad[:, :width])  1.25 us

profile of v2, /device:TPU:0, one launch (start us, length us, event | category | flops | bytes accessed | tf_op | source)
XLA Modules:
  0.0 56.6 jit_solution(11445855912591254185)
XLA Ops:
  0.6 54.1 %relay.1 = (bf16[48,8192]{1,0:T(8,128)(2,1)S(1)}, f32[1,8192]{1,0:T(1,128)S(1)}) custom-call(s32[1,8]{1,0:T(1,128)} %len_hbm.1, s32[8,16]{1,0:T(8,128)} %bitcast.12, bf16[1,8192]{1,0:T(2,128)(2,1)} %gain_hbm.1, bf16[128,8192]{1,0:T(8,128)(2,1)} %bitcast.8, bf16[128,8192]{1,0:T(8,128)(2,1)} %bitcast.9, bf16[48,8192]{1,0:T(8,128)(2,1)} %bitcast.10, ...), custom_call_target="tpu_custom_call" | custom-call | tf_op jit(solution)/shard_map/relay/pallas_call | solution.py:477
  54.7 1.2 %bitcast_convert_fusion = f32[1,48,8192]{2,1,0:T(8,128)} fusion(bf16[48,8192]{1,0:T(8,128)(2,1)S(1)} %get-tuple-element.4), kind=kLoop, calls=%fused_computation | loop fusion | flops 393216 | bytes 2359296 | tf_op jit(solution)/shard_map/convert_element_type | solution.py:487
  56.0 0.6 %copy.10 = f32[1,8192]{1,0:T(1,128)} copy(f32[1,8192]{1,0:T(1,128)S(1)} %get-tuple-element.9) | data formatting | bytes 65536

commit v3 on v2

--- a/solution.py
+++ b/solution.py
@@ -84,14 +84,16 @@
 
 def kernel(sizes, len_hbm, keep_hbm, gain_hbm, e_hbm, g_hbm, d_hbm, u_hbm, out_ref, gout_ref,
            len_ref, keep_ref, gain_ref, e_ref, g_ref, d_ref, u_ref, every, own_all, gram_tx, gram_rx, gram_all,
-           tx, ttx, xrx, txrx, ztx, tztx, zrx, tzrx, mix_tx, mix_xrx, mix_ztx, mix_zrx, arx, tarx,
-           load_sem, s1, r1, f1, s2, r2, s3, r3, s4, r4, sx, rx, stx, rtx, sz, rz, stz, rtz,
-           smx, rmx, smz, rmz, sa, ra, sta, rta, sf, rf, stf, rtf):
+           tx, xrx, ztx, zrx, hold, gtx, grx, garx, mix_tx, mix_xrx, mix_ztx, mix_zrx, mix_all, arx,
+           load_sem, s1, r1, f1, s2, r2, s3, r3, s4, r4, sx, rx, sz, rz, sg, rg, sga, rga,
+           smx, rmx, smz, rmz, smb, rmb, saz, raz, sax, rax):
     total, groups, inner, rank, micro, tok, width, part, model = sizes
     rows = micro * tok
     outer = groups // inner
     chunks = width // part
-    tiles = part // 128
+    halves = 2 if part % 256 == 0 and part > 256 else 1
+    sub = part // halves
+    tiles = sub // 128
     bf, f32 = jnp.bfloat16, jnp.float32
     my = lax.axis_index("section")
     me = lax.axis_index("dp")
@@ -258,145 +260,198 @@
                             jnp.concatenate([jnp.zeros_like(lam), lam], axis=1)], axis=0)
 
     peer = me + 1 - 2 * x
+    near_end = jnp.minimum(z, outer - 1 - z)
+    lead = outer - 1 - 2 * near_end
+
+    def far(k):
+        j = jnp.maximum(k - lead, 0)
+        inner_q = jnp.where(j % 2 == 0, 2 * near_end - j // 2, j // 2)
+        q = jnp.where(k < lead, outer - 1 - k, inner_q)
+        return jnp.where(z > near_end, outer - 1 - q, q)
+
+    def columns(c, h):
+        return pl.ds(pl.multiple_of(c * part + h * sub, sub), sub)
+
+    def piece(c, h):
+        at = columns(c, h)
+        both = mm(left, jnp.concatenate([g_ref[:, at], e_ref[:, at]], axis=0))
+        row = jnp.sum(d_ref[:, at].astype(f32) * both[rank:], axis=0, keepdims=True)
+        return both[:rank], row
+
+    def put_row(c, h, row):
+        for i in range(tiles):
+            gtx[c, h * tiles + i:h * tiles + i + 1, :] = row[:, 128 * i:128 * (i + 1)]
+
+    def mix_x():
+        return remote(mix_tx.at[1 - x], mix_xrx, smx, rmx, dp=peer)
+
+    def mix_z(q, src):
+        return remote(mix_ztx, mix_zrx.at[src], smz.at[q], rmz.at[src], dp=q * inner + x)
+
+    def mix_back(side):
+        return remote(mix_all.at[side], mix_all.at[side], smb, rmb, dp=peer)
+
+    def send_x(p):
+        return remote(tx.at[p], xrx.at[p], sx.at[p], rx.at[p], dp=peer)
+
+    def send_z(way, p):
+        return remote(ztx.at[p], zrx.at[way, p], sz.at[p], rz.at[way, p], dp=(z + 1 - 2 * way) * inner + x)
+
+    def send_row(c, src):
+        return remote(gtx.at[c], grx.at[src], sg.at[c], rg.at[src], dp=c)
+
+    def give_z(way, p):
+        return remote(arx.at[p], arx.at[p], saz.at[way, p], raz.at[p], dp=(z + 1 - 2 * way) * inner + x)
+
+    def give_x(p):
+        return remote(arx.at[p], arx.at[p], sax.at[p], rax.at[p], dp=peer)
+
+    def give_row(j, src):
+        return remote(garx.at[src], garx.at[src], sga.at[j], rga.at[src], dp=j)
+
     mix_tx[0] = mix.astype(bf)
     mix_tx[1] = v.astype(bf)
-
-    def mix_x():
-        return remote(mix_tx, mix_xrx, smx, rmx, dp=peer)
-
-    def mix_z(j, src):
-        return remote(mix_ztx, mix_zrx.at[src], smz.at[j], rmz.at[src], dp=j * inner + x)
-
-    def piece(c):
-        e = e_ref[:, lanes(c)]
-        both = mm(left, jnp.concatenate([g_ref[:, lanes(c)], e], axis=0))
-        row = jnp.sum(d_ref[:, lanes(c)].astype(f32) * both[rank:], axis=0, keepdims=True)
-        return both[:rank], row
-
-    def put_row(ref, row):
-        for i in range(tiles):
-            ref[i:i + 1, :] = row[:, 128 * i:128 * (i + 1)]
-
-    def send_x(q):
-        return (remote(tx.at[q], xrx.at[q], sx.at[q], rx.at[q], dp=peer),
-                remote(ttx.at[q], txrx.at[q], stx.at[q], rtx.at[q], dp=peer))
-
-    def send_z(q, src):
-        return (remote(ztx.at[q], zrx.at[src], sz.at[q], rz.at[src], dp=q * inner + x),
-                remote(tztx.at[q], tzrx.at[src], stz.at[q], rtz.at[src], dp=q * inner + x))
-
-    if inner > 1:
-        mix_x().start()
-
-        def first(k, carry):
-            q = (z + 1 + k) % outer
-            c = q * inner + 1 - x
-            big, row = piece(jnp.minimum(c, chunks - 1))
-            tx[q] = big.astype(bf)
-            put_row(ttx.at[q], row)
-            for copy in send_x(q):
-                copy.start()
-            return carry
-
-        lax.fori_loop(0, outer, first, 0)
-        mix_x().wait_recv()
-        for i in range(2):
-            mix_ztx[i] = (mix_tx[i].astype(f32) + mix_xrx[i].astype(f32)).astype(bf)
-    else:
-        mix_ztx[...] = mix_tx[...]
+    mix_x().start()
+
+    def first(k, carry):
+        q = far(k)
+        c = q * inner + 1 - x
+        for h in range(halves):
+            big, row = piece(jnp.minimum(c, chunks - 1), h)
+            tx[q * halves + h] = big.astype(bf)
+            put_row(c, h, row)
+            send_x(q * halves + h).start()
+        send_row(c, me).start()
+        return carry
+
+    lax.fori_loop(0, outer, first, 0)
+    mix_x().wait_recv()
+    mix_ztx[...] = (mix_tx[x].astype(f32) + mix_xrx[...].astype(f32)).astype(bf)
     for k in range(1, outer):
         mix_z((z + k) % outer, z).start()
 
     def second(k, carry):
-        q = (z + 1 + k) % outer
-        big, row = piece(jnp.minimum(q * inner + x, chunks - 1))
-        put_row(tztx.at[q], row)
-        if inner > 1:
-            for copy in send_x(q):
-                copy.wait_recv()
-            big = big + xrx[q].astype(f32)
-            tztx[q, :tiles] = tztx[q, :tiles] + txrx[q, :tiles]
-        ztx[q] = big.astype(bf)
-
-        @pl.when(k < outer - 1)
-        def _():
-            for copy in send_z(q, z):
-                copy.start()
-        return carry
-
-    lax.fori_loop(0, outer, second, 0)
-
-    wait_weights(0)
-    mixed = [mix_ztx[i].astype(f32) for i in range(2)]
+        q = far(k)
+        c = q * inner + x
+        way = jnp.where(q > z, 0, 1)
+        behind = jnp.where(q > z, z, outer - 1 - z)
+        for h in range(halves):
+            p = q * halves + h
+            big, row = piece(jnp.minimum(c, chunks - 1), h)
+            put_row(c, h, row)
+            send_x(p).wait_recv()
+            hold[...] = big + xrx[p].astype(f32)
+
+            @pl.when(behind > 0)
+            def _():
+                send_z(way, p).wait_recv()
+                hold[...] = hold[...] + zrx[way, p].astype(f32)
+
+            ztx[p] = hold[...].astype(bf)
+            send_z(way, p).start()
+        send_row(c, me).start()
+        return carry
+
+    lax.fori_loop(0, outer - 1, second, 0)
+
+    mixed = mix_ztx[...].astype(f32)
     for k in range(1, outer):
         q = (z + k) % outer
         mix_z(z, q).wait_recv()
-        mixed = [mixed[i] + mix_zrx[q, i].astype(f32) for i in range(2)]
-    col = lax.broadcasted_iota(jnp.int32, (rank, total * rank), 1)
-    low = jnp.where(col < my * rank, mixed[0], 0.0).astype(bf)
-    high = jnp.where(col < my * rank, 0.0, mixed[0]).astype(bf)
-    big = mm(high, every[0]) + mm(mixed[1].astype(bf), every[1]) + ztx[z].astype(f32)
-    row = jnp.sum(d_ref[:, lanes(mine)].astype(f32) * mm(low, every[1]), axis=0, keepdims=True)
-    put_row(tarx.at[me], row)
-    tall = tarx[me, :tiles] + tztx[z, :tiles]
-    for k in range(1, outer):
-        q = (z + k) % outer
-        for copy in send_z(z, q):
-            copy.wait_recv()
-        big = big + zrx[q].astype(f32)
-        tall = tall + tzrx[q, :tiles]
-    tarx[me, :tiles] = tall
-    arx[me] = big.astype(bf)
-
-    def gather_z(j, src):
-        c = src * inner + x
-        return (remote(arx.at[c], arx.at[c], sa.at[j], ra.at[src], dp=j * inner + x),
-                remote(tarx.at[c], tarx.at[c], sta.at[j], rta.at[src], dp=j * inner + x))
-
-    def gather_x(q, side):
-        c = q * inner + side
-        return (remote(arx.at[c], arx.at[c], sf.at[q], rf.at[q], dp=peer),
-                remote(tarx.at[c], tarx.at[c], stf.at[q], rtf.at[q], dp=peer))
-
-    def write(c):
+        mixed = mixed + mix_zrx[q].astype(f32)
+    mix_all[x] = mixed.astype(bf)
+    mix_back(x).start()
+    wait_weights(0)
+    mine_parts = [piece(mine, h) for h in range(halves)]
+    mix_back(1 - x).wait_recv()
+    low = jnp.where(col < my * rank, mix_all[0].astype(f32), 0.0).astype(bf)
+    high = jnp.where(col < my * rank, 0.0, mix_all[0].astype(f32)).astype(bf)
+    for h in range(halves):
+        big, row = mine_parts[h]
+        p = z * halves + h
+        at = slice(h * sub, (h + 1) * sub)
+        big = big + mm(high, every[0, :, at]) + mm(mix_all[1], every[1, :, at])
+        row = row + jnp.sum(d_ref[:, columns(mine, h)].astype(f32) * mm(low, every[1, :, at]), axis=0, keepdims=True)
+        put_row(me, h, row)
+        send_x(p).wait_recv()
+        hold[...] = big + xrx[p].astype(f32)
+        for way, behind in ((0, z), (1, outer - 1 - z)):
+            @pl.when(behind > 0)
+            def _():
+                send_z(way, p).wait_recv()
+                hold[...] = hold[...] + zrx[way, p].astype(f32)
+
+        p = me * halves + h
+        arx[p] = hold[...].astype(bf)
+        for way, behind in ((0, outer - 1 - z), (1, z)):
+            @pl.when(behind > 0)
+            def _():
+                give_z(way, p).start()
+
+        give_x(p).start()
+
+    def add_row(k, acc):
+        src = (me + k) % groups
+        send_row(me, src).wait_recv()
+        return acc + grx[src]
+
+    garx[me] = lax.fori_loop(1, groups, add_row, gtx[me])
+
+    def spread_row(k, carry):
+        give_row((me + k) % groups, me).start()
+        return carry
+
+    lax.fori_loop(1, groups, spread_row, 0)
+
+    def write(c, h):
         def go():
-            out_ref[:, lanes(c)] = arx[c]
-            for i in range(tiles):
-                gout_ref[:, pl.ds(pl.multiple_of(c * part + 128 * i, 128), 128)] = tarx[c, i:i + 1, :]
+            out_ref[:, columns(c, h)] = arx[c * halves + h]
         if chunks == groups:
             go()
         else:
             pl.when(c < chunks)(go)
 
-    for k in range(1, outer):
-        for copy in gather_z((z + k) % outer, z):
-            copy.start()
-    if inner > 1:
-        for copy in gather_x(z, x):
-            copy.start()
-    write(me)
-
     def pass_on(k, carry):
-        q = (z + k) % outer
-        for copy in gather_z(z, q):
-            copy.wait_recv()
-        if inner > 1:
-            for copy in gather_x(q, x):
-                copy.start()
-        write(q * inner + x)
-        return carry
-
-    lax.fori_loop(1, outer, pass_on, 0)
-
-    if inner > 1:
-        def last(k, carry):
-            q = (z + k) % outer
-            for copy in gather_x(q, 1 - x):
-                copy.wait_recv()
-            write(q * inner + 1 - x)
-            return carry
-
-        lax.fori_loop(0, outer, last, 0)
+        q = far(outer - 2 - k)
+        c = q * inner + x
+        way = jnp.where(q < z, 0, 1)
+        ahead = jnp.where(q < z, outer - 1 - z, z)
+        for h in range(halves):
+            p = c * halves + h
+            give_z(way, p).wait_recv()
+
+            @pl.when(ahead > 0)
+            def _():
+                give_z(way, p).start()
+
+            give_x(p).start()
+            write(c, h)
+        return carry
+
+    lax.fori_loop(0, outer - 1, pass_on, 0)
+    for h in range(halves):
+        write(me, h)
+
+    def write_row(c, carry):
+        for i in range(part // 128):
+            gout_ref[:, pl.ds(pl.multiple_of(c * part + 128 * i, 128), 128)] = garx[c, i:i + 1, :]
+        return carry
+
+    def wait_row(k, carry):
+        give_row(me, (me + k) % groups).wait_recv()
+        return carry
+
+    lax.fori_loop(1, groups, wait_row, 0)
+    lax.fori_loop(0, chunks, write_row, 0)
+
+    def last(k, carry):
+        c = far(outer - 1 - k) * inner + 1 - x
+        for h in range(halves):
+            give_x(c * halves + h).wait_recv()
+            write(c, h)
+        return carry
+
+    lax.fori_loop(0, outer, last, 0)
 
     for w in range(2):
         for k in range(step, total, step):
@@ -409,9 +464,20 @@
         j = (my + k) % total
         owns(j, my).wait_send()
         all_grams(j, my).wait_send()
+    mix_x().wait_send()
+    mix_back(x).wait_send()
+    for h in range(halves):
+        p = me * halves + h
+        for way, behind in ((0, outer - 1 - z), (1, z)):
+            @pl.when(behind > 0)
+            def _():
+                give_z(way, p).wait_send()
 
     def left_dp(k, carry):
-        grams((me + k) % groups, me).wait_send()
+        j = (me + k) % groups
+        grams(j, me).wait_send()
+        send_row(j, me).wait_send()
+        give_row(j, me).wait_send()
         return carry
 
     lax.fori_loop(1, groups, left_dp, 0)
@@ -419,20 +485,24 @@
     def left_z(k, carry):
         q = (z + k) % outer
         mix_z(q, z).wait_send()
-        for copy in send_z(q, z) + gather_z(q, z):
-            copy.wait_send()
+        ahead = jnp.where(q < z, outer - 1 - z, z)
+        for h in range(halves):
+            send_z(jnp.where(q > z, 0, 1), q * halves + h).wait_send()
+
+            @pl.when(ahead > 0)
+            def _():
+                give_z(jnp.where(q < z, 0, 1), (q * inner + x) * halves + h).wait_send()
         return carry
 
     lax.fori_loop(1, outer, left_z, 0)
-    if inner > 1:
-        mix_x().wait_send()
-
-        def left_x(q, carry):
-            for copy in send_x(q) + gather_x(q, x):
-                copy.wait_send()
-            return carry
-
-        lax.fori_loop(0, outer, left_x, 0)
+
+    def left_x(q, carry):
+        for h in range(halves):
+            send_x(q * halves + h).wait_send()
+            give_x((q * inner + x) * halves + h).wait_send()
+        return carry
+
+    lax.fori_loop(0, outer, left_x, 0)
 
 
 def body(entry, gain, down, up, gout, lengths, keep):
@@ -445,7 +515,9 @@
     part = 128 * (-(-width // (128 * groups)))
     pad = -width % part
     wide = width + pad
-    inner = 2 if groups % 2 == 0 else 1
+    inner = 2
+    halves = 2 if part % 256 == 0 and part > 256 else 1
+    sub = part // halves
     outer = groups // inner
     widen = lambda a: jnp.pad(a, ((0, 0), (0, pad))) if pad else a
     hold = lambda a: pltpu.with_memory_space_constraint(a, pltpu.HBM)
@@ -453,24 +525,28 @@
     go = hold(widen(gout[0].reshape(rows, width)))
     d, u = hold(widen(down[0])), hold(widen(up[0]))
     tall = max(8, part // 128)
+    pieces = outer * halves
     sizes = (total, groups, inner, rank, micro, tok, wide, part, width)
     vm = lambda *s, t=bf: pltpu.VMEM(s, t)
     dma = lambda *n: pltpu.SemaphoreType.DMA(n)
+    one = pltpu.SemaphoreType.DMA
     scratch = [
         pltpu.SMEM((1, micro), jnp.int32), vm(micro, tok, t=jnp.int32), vm(1, wide),
         vm(rows, wide), vm(rows, wide), vm(rank, wide), vm(rank, wide),
         vm(2, total * rank, part),
         vm(total, 3 * rank + 16, rows, t=f32),
         vm(rank, total * rank), vm(groups, rank, total * rank), vm(total * rank, total * rank),
-        vm(outer, rank, part), vm(outer, tall, 128, t=f32), vm(outer, rank, part), vm(outer, tall, 128, t=f32),
-        vm(outer, rank, part), vm(outer, tall, 128, t=f32), vm(outer, rank, part), vm(outer, tall, 128, t=f32),
-        vm(2, rank, total * rank), vm(2, rank, total * rank), vm(2, rank, total * rank),
-        vm(outer, 2, rank, total * rank),
-        vm(groups, rank, part), vm(groups, tall, 128, t=f32),
-        dma(8), dma(2, total), dma(2, total), dma(2, total), dma(total), dma(total), dma(groups), dma(groups), dma(total), dma(total),
-        dma(outer), dma(outer), dma(outer), dma(outer), dma(outer), dma(outer), dma(outer), dma(outer),
-        pltpu.SemaphoreType.DMA, pltpu.SemaphoreType.DMA, dma(outer), dma(outer),
-        dma(outer), dma(outer), dma(outer), dma(outer), dma(outer), dma(outer), dma(outer), dma(outer),
+        vm(pieces, rank, sub), vm(pieces, rank, sub), vm(pieces, rank, sub), vm(2, pieces, rank, sub),
+        vm(rank, sub, t=f32),
+        vm(groups, tall, 128, t=f32), vm(groups, tall, 128, t=f32), vm(groups, tall, 128, t=f32),
+        vm(2, rank, total * rank), vm(rank, total * rank), vm(rank, total * rank),
+        vm(outer, rank, total * rank), vm(2, rank, total * rank),
+        vm(groups * halves, rank, sub),
+        dma(8), dma(2, total), dma(2, total), dma(2, total), dma(total), dma(total), dma(groups), dma(groups),
+        dma(total), dma(total),
+        dma(pieces), dma(pieces), dma(pieces), dma(2, pieces), dma(groups), dma(groups), dma(groups), dma(groups),
+        one, one, dma(outer), dma(outer), one, one,
+        dma(2, groups * halves), dma(groups * halves), dma(groups * halves), dma(groups * halves),
     ]
     inside = pl.BlockSpec(memory_space=pltpu.VMEM)
     outside = pl.BlockSpec(memory_space=pltpu.HBM)

time: 57.4 us -> 54.6 us (0.951); the launches traced: 56.6 us -> 54.4 us
  Pallas kernels: 54.1 us -> 51.9 us
    pallas_call x1, Pallas kernels: 54.1 us -> 51.9 us  [body(): pl.pallas_call(functools.partial(kernel, sizes), out_shape=(jax.ShapeDtyp...]
where the time goes in v3:
time: 54.6 us; the launch traced here: 54.4 us
  Pallas kernels  51.9 us (95%)
  other arithmetic  1.25 us (2%)
  between operations  0.64 us (1%)
  local copies, waits for them, and re-layouts  0.61 us (1%)
    pallas_call x1, Pallas kernels, body(): pl.pallas_call(functools.partial(kernel, sizes), out_shape=(jax.ShapeDtyp...  51.9 us
    convert_element_type x1, other arithmetic, body(): return (up_grad[None, :, :width].astype(f32), gain_grad[:, :width])  1.25 us

profile of v3, /device:TPU:0, one launch (start us, length us, event | category | flops | bytes accessed | tf_op | source)
XLA Modules:
  0.0 54.4 jit_solution(13813683161246863100)
XLA Ops:
  0.6 51.9 %relay.1 = (bf16[48,8192]{1,0:T(8,128)(2,1)S(1)}, f32[1,8192]{1,0:T(1,128)S(1)}) custom-call(s32[1,8]{1,0:T(1,128)} %len_hbm.1, s32[8,16]{1,0:T(8,128)} %bitcast.12, bf16[1,8192]{1,0:T(2,128)(2,1)} %gain_hbm.1, bf16[128,8192]{1,0:T(8,128)(2,1)} %bitcast.8, bf16[128,8192]{1,0:T(8,128)(2,1)} %bitcast.9, bf16[48,8192]{1,0:T(8,128)(2,1)} %bitcast.10, ...), custom_call_target="tpu_custom_call" | custom-call | tf_op jit(solution)/shard_map/relay/pallas_call | solution.py:553
  52.6 1.2 %bitcast_convert_fusion = f32[1,48,8192]{2,1,0:T(8,128)} fusion(bf16[48,8192]{1,0:T(8,128)(2,1)S(1)} %get-tuple-element.4), kind=kLoop, calls=%fused_computation | loop fusion | flops 393216 | bytes 2359296 | tf_op jit(solution)/shard_map/convert_element_type | solution.py:563
  53.8 0.6 %copy.10 = f32[1,8192]{1,0:T(1,128)} copy(f32[1,8192]{1,0:T(1,128)S(1)} %get-tuple-element.9) | data formatting | bytes 65536

commit v4 on v3

--- a/solution.py
+++ b/solution.py
@@ -84,8 +84,8 @@
 
 def kernel(sizes, len_hbm, keep_hbm, gain_hbm, e_hbm, g_hbm, d_hbm, u_hbm, out_ref, gout_ref,
            len_ref, keep_ref, gain_ref, e_ref, g_ref, d_ref, u_ref, every, own_all, gram_tx, gram_rx, gram_all,
-           tx, xrx, ztx, zrx, hold, gtx, grx, garx, mix_tx, mix_xrx, mix_ztx, mix_zrx, mix_all, arx,
-           load_sem, s1, r1, f1, s2, r2, s3, r3, s4, r4, sx, rx, sz, rz, sg, rg, sga, rga,
+           tx, xrx, ztx, zrx, zend, gtx, grx, garx, mix_tx, mix_xrx, mix_ztx, mix_zrx, mix_all, arx,
+           load_sem, s1, r1, rm, s2, r2, s3, r3, s4, r4, sx, rx, sz, rz, rze, sg, rg, sga, rga,
            smx, rmx, smz, rmz, smb, rmb, saz, raz, sax, rax):
     total, groups, inner, rank, micro, tok, width, part, model = sizes
     rows = micro * tok
@@ -131,12 +131,45 @@
         return pltpu.make_async_remote_copy(src_ref=src, dst_ref=dst, send_sem=send, recv_sem=recv,
                                             device_id=where, device_id_type=MESH)
 
-    for i in range(4):
-        loads[i].wait()
     real = jnp.where(me < chunks, 1.0, 0.0).astype(f32)
+    loads[0].wait()
     if chunks < groups:
         every[1, ranks(my), :] = (every[1, ranks(my), :].astype(f32) * real).astype(bf)
-
+    pl.semaphore_wait(barrier, total + groups - 2)
+
+    step = 2 if total % 2 == 0 else 1
+    mate = my + 1 - 2 * (my % 2)
+
+    def block(w, src):
+        return every.at[w, ranks(src), :]
+
+    def weights(w, j, src):
+        return remote(block(w, src), block(w, src), s1, r1.at[w, src // step], section=j)
+
+    def share(w, src):
+        return remote(block(w, src), block(w, src), s1, rm.at[w], section=mate)
+
+    def send_weights(w):
+        for k in range(step, total, step):
+            weights(w, (my + k) % total, my).start()
+        if step == 2:
+            share(w, my).start()
+
+    def pass_weights(w):
+        for k in range(step, total, step):
+            src = (my + k) % total
+            weights(w, my, src).wait_recv()
+            if step == 2:
+                share(w, src).start()
+
+    def wait_weights(w):
+        if step == 2:
+            part_of = every.at[w, pl.ds(0, total // 2 * rank), :]
+            remote(part_of, part_of, s1, rm.at[w], section=mate).wait_recv()
+
+    send_weights(1)
+    for i in range(1, 4):
+        loads[i].wait()
     lane = lax.broadcasted_iota(jnp.int32, (1, rows), 1)
     valid = jnp.zeros((1, rows), f32)
     for m in range(micro):
@@ -151,39 +184,6 @@
         spread = spread + jnp.where(lane16 == row16 + m * tok, 1.0, 0.0)
     kept_row = valid * jnp.sum(mm(keep_ref[...].astype(f32), spread) * member, axis=0, keepdims=True)
 
-    pl.semaphore_wait(barrier, total + groups - 2)
-
-    step = 2 if total % 2 == 0 else 1
-    mate = my + 1 - 2 * (my % 2)
-
-    def block(w, src):
-        return every.at[w, ranks(src), :]
-
-    def weights(w, j, src):
-        return remote(block(w, src), block(w, src), s1.at[w, j], r1.at[w, src], section=j)
-
-    def share(w, src):
-        return remote(block(w, src), block(w, src), f1.at[w, src], r1.at[w, src], section=mate)
-
-    def send_weights(w):
-        for k in range(step, total, step):
-            weights(w, (my + k) % total, my).start()
-        if step == 2:
-            weights(w, mate, my).start()
-
-    def pass_weights(w):
-        for k in range(step, total, step):
-            src = (my + k) % total
-            weights(w, my, src).wait_recv()
-            if step == 2:
-                share(w, src).start()
-
-    def wait_weights(w):
-        if step == 2:
-            for k in range(0, total, 2):
-                weights(w, my, (mate + k) % total).wait_recv()
-
-    send_weights(1)
     for i in range(4, 7):
         loads[i].wait()
 
@@ -196,20 +196,15 @@
     zero = jnp.zeros((rank, rows), f32)
     sums = (jnp.zeros((2 * rank, rows), f32), jnp.zeros((8, rows), f32))
     aue, nn = lax.fori_loop(0, chunks, entry_chunk, sums)
-    loads[7].wait()
-    ug = lax.fori_loop(0, chunks, lambda c, acc: acc + mm(u_ref[:, lanes(c)], g_ref[:, lanes(c)], NT), zero)
-    own_all[my] = jnp.concatenate([aue, ug, nn, jnp.broadcast_to(kept_row, (8, rows))], axis=0)
-
-    def owns(j, src):
-        return remote(own_all.at[src], own_all.at[src], s2.at[j], r2.at[src], section=j)
-
-    for k in range(1, total):
-        owns((my + k) % total, my).start()
     every[0, ranks(my), :] = (d_ref[:, lanes(mine)].astype(f32) * gain_ref[:, lanes(mine)].astype(f32)
                               * real).astype(bf)
-    send_weights(0)
-
     pass_weights(1)
+    loads[7].wait()
+
+    def out_chunk(c, acc):
+        return acc + mm(u_ref[:, lanes(c)], g_ref[:, lanes(c)], NT)
+
+    ug = lax.fori_loop(0, chunks // 2, out_chunk, zero)
     wait_weights(1)
     size = total * rank
     col = lax.broadcasted_iota(jnp.int32, (rank, size), 1)
@@ -217,33 +212,40 @@
     gram_tx[...] = jnp.where(col < my * rank, both[:rank], both[rank:]).astype(bf)
 
     def grams(j, src):
-        return remote(gram_tx, gram_rx.at[src], s3.at[j], r3.at[src], dp=j)
+        return remote(gram_tx, gram_rx.at[src], s3, r3, dp=j)
 
     def send_gram(k, c):
         grams((me + k) % groups, me).start()
         return c
 
     lax.fori_loop(1, groups, send_gram, 0)
-    pass_weights(0)
     gram_rx[me] = gram_tx[...]
-
-    def wait_gram(k, c):
-        grams(me, (me + k) % groups).wait_recv()
-        return c
-
-    lax.fori_loop(1, groups, wait_gram, 0)
+    ug = lax.fori_loop(chunks // 2, chunks, out_chunk, ug)
+    own_all[my] = jnp.concatenate([aue, ug, nn, jnp.broadcast_to(kept_row, (8, rows))], axis=0)
+
+    def owns(j, src):
+        return remote(own_all.at[src], own_all.at[src], s2, r2, section=j)
+
+    for k in range(1, total):
+        owns((my + k) % total, my).start()
+    others = gram_rx.at[pl.ds(0, groups - 1)]
+    all_of_grams = remote(others, others, s3, r3, dp=me)
+    all_of_grams.wait_recv()
     gram = lax.fori_loop(0, groups, lambda k, acc: acc + gram_rx[k].astype(f32), jnp.zeros((rank, size), f32))
     gram_all[ranks(my), :] = gram.astype(bf)
 
     def all_grams(j, src):
-        return remote(gram_all.at[ranks(src), :], gram_all.at[ranks(src), :], s4.at[j], r4.at[src], section=j)
+        return remote(gram_all.at[ranks(src), :], gram_all.at[ranks(src), :], s4, r4, section=j)
 
     for k in range(1, total):
         all_grams((my + k) % total, my).start()
-    for k in range(1, total):
-        owns(my, (my + k) % total).wait_recv()
-    for k in range(1, total):
-        all_grams(my, (my + k) % total).wait_recv()
+    send_weights(0)
+    others = own_all.at[pl.ds(0, total - 1)]
+    all_of_owns = remote(others, others, s2, r2, section=my)
+    all_of_owns.wait_recv()
+    others = gram_all.at[pl.ds(0, (total - 1) * rank), :]
+    all_of_tables = remote(others, others, s4, r4, section=my)
+    all_of_tables.wait_recv()
 
     table = gram_all[...]
     eye = jnp.where(lax.broadcasted_iota(jnp.int32, (size, size), 0)
@@ -260,14 +262,15 @@
                             jnp.concatenate([jnp.zeros_like(lam), lam], axis=1)], axis=0)
 
     peer = me + 1 - 2 * x
-    near_end = jnp.minimum(z, outer - 1 - z)
-    lead = outer - 1 - 2 * near_end
-
-    def far(k):
-        j = jnp.maximum(k - lead, 0)
-        inner_q = jnp.where(j % 2 == 0, 2 * near_end - j // 2, j // 2)
-        q = jnp.where(k < lead, outer - 1 - k, inner_q)
-        return jnp.where(z > near_end, outer - 1 - q, q)
+    twin = z + 1 - 2 * (z % 2)
+    pairs = outer // 2
+
+    def across(k, side):
+        return 2 * ((z // 2 + 1 + k) % pairs) + side
+
+    def order(k):
+        own_side = jnp.where(k < outer - 2, across(k - pairs + 1, z % 2), jnp.where(k < outer - 1, twin, z))
+        return jnp.where(k < pairs - 1, across(k, twin % 2), own_side)
 
     def columns(c, h):
         return pl.ds(pl.multiple_of(c * part + h * sub, sub), sub)
@@ -286,81 +289,99 @@
         return remote(mix_tx.at[1 - x], mix_xrx, smx, rmx, dp=peer)
 
     def mix_z(q, src):
-        return remote(mix_ztx, mix_zrx.at[src], smz.at[q], rmz.at[src], dp=q * inner + x)
+        return remote(mix_ztx, mix_zrx.at[src], smz, rmz, dp=q * inner + x)
 
     def mix_back(side):
         return remote(mix_all.at[side], mix_all.at[side], smb, rmb, dp=peer)
 
     def send_x(p):
-        return remote(tx.at[p], xrx.at[p], sx.at[p], rx.at[p], dp=peer)
-
-    def send_z(way, p):
-        return remote(ztx.at[p], zrx.at[way, p], sz.at[p], rz.at[way, p], dp=(z + 1 - 2 * way) * inner + x)
-
-    def send_row(c, src):
-        return remote(gtx.at[c], grx.at[src], sg.at[c], rg.at[src], dp=c)
-
-    def give_z(way, p):
-        return remote(arx.at[p], arx.at[p], saz.at[way, p], raz.at[p], dp=(z + 1 - 2 * way) * inner + x)
-
-    def give_x(p):
-        return remote(arx.at[p], arx.at[p], sax.at[p], rax.at[p], dp=peer)
-
-    def give_row(j, src):
-        return remote(garx.at[src], garx.at[src], sga.at[j], rga.at[src], dp=j)
+        return remote(tx.at[p], xrx.at[p], sx, rx.at[p], dp=peer)
+
+    def send_end(q, h, src):
+        return remote(ztx.at[q * halves + h], zend.at[src * halves + h], sz, rze.at[src * halves + h], dp=q * inner + x)
+
+    def send_twin(p):
+        return remote(ztx.at[p], zrx.at[p], sz, rz.at[p], dp=twin * inner + x)
+
+    def send_row(c):
+        return remote(gtx.at[c], grx.at[me], sg, rg, dp=c)
+
+    def give_z(q, src, h):
+        p = (src * inner + x) * halves + h
+        return remote(arx.at[p], arx.at[p], saz, raz.at[src * halves + h], dp=q * inner + x)
+
+    def give_x(q, side, h):
+        p = (q * inner + side) * halves + h
+        return remote(arx.at[p], arx.at[p], sax, rax.at[q * halves + h], dp=peer)
+
+    def give_row(j):
+        return remote(garx.at[me], garx.at[me], sga, rga, dp=j)
+
+    def batch(ref, count, send, recv):
+        some = ref.at[pl.ds(0, count)]
+        return remote(some, some, send, recv, dp=peer)
 
     mix_tx[0] = mix.astype(bf)
     mix_tx[1] = v.astype(bf)
     mix_x().start()
 
     def first(k, carry):
-        q = far(k)
+        q = order(k)
         c = q * inner + 1 - x
         for h in range(halves):
             big, row = piece(jnp.minimum(c, chunks - 1), h)
             tx[q * halves + h] = big.astype(bf)
             put_row(c, h, row)
             send_x(q * halves + h).start()
-        send_row(c, me).start()
+        send_row(c).start()
         return carry
 
     lax.fori_loop(0, outer, first, 0)
+    pass_weights(0)
     mix_x().wait_recv()
     mix_ztx[...] = (mix_tx[x].astype(f32) + mix_xrx[...].astype(f32)).astype(bf)
     for k in range(1, outer):
         mix_z((z + k) % outer, z).start()
 
-    def second(k, carry):
-        q = far(k)
+    def gather_part(q, h):
         c = q * inner + x
-        way = jnp.where(q > z, 0, 1)
-        behind = jnp.where(q > z, z, outer - 1 - z)
+        big, row = piece(jnp.minimum(c, chunks - 1), h)
+        put_row(c, h, row)
+        send_x(q * halves + h).wait_recv()
+        return big + xrx[q * halves + h].astype(f32)
+
+    def to_twin(k, carry):
+        q = across(k, twin % 2)
+        for h in range(halves):
+            ztx[q * halves + h] = gather_part(q, h).astype(bf)
+            send_twin(q * halves + h).start()
+        send_row(q * inner + x).start()
+        return carry
+
+    def to_end(k, carry):
+        q = across(k, z % 2)
         for h in range(halves):
             p = q * halves + h
-            big, row = piece(jnp.minimum(c, chunks - 1), h)
-            put_row(c, h, row)
-            send_x(p).wait_recv()
-            hold[...] = big + xrx[p].astype(f32)
-
-            @pl.when(behind > 0)
-            def _():
-                send_z(way, p).wait_recv()
-                hold[...] = hold[...] + zrx[way, p].astype(f32)
-
-            ztx[p] = hold[...].astype(bf)
-            send_z(way, p).start()
-        send_row(c, me).start()
-        return carry
-
-    lax.fori_loop(0, outer - 1, second, 0)
+            big = gather_part(q, h)
+            send_twin(p).wait_recv()
+            ztx[p] = (big + zrx[p].astype(f32)).astype(bf)
+            send_end(q, h, z).start()
+        send_row(q * inner + x).start()
+        return carry
+
+    lax.fori_loop(0, pairs - 1, to_twin, 0)
+    lax.fori_loop(0, pairs - 1, to_end, 0)
 
     mixed = mix_ztx[...].astype(f32)
-    for k in range(1, outer):
-        q = (z + k) % outer
-        mix_z(z, q).wait_recv()
-        mixed = mixed + mix_zrx[q].astype(f32)
+    batch(mix_zrx, outer - 1, smz, rmz).wait_recv()
+    mixed = lax.fori_loop(1, outer, lambda k, acc: acc + mix_zrx[(z + k) % outer].astype(f32), mixed)
     mix_all[x] = mixed.astype(bf)
     mix_back(x).start()
+
+    for h in range(halves):
+        ztx[twin * halves + h] = gather_part(twin, h).astype(bf)
+        send_end(twin, h, z).start()
+    send_row(twin * inner + x).start()
     wait_weights(0)
     mine_parts = [piece(mine, h) for h in range(halves)]
     mix_back(1 - x).wait_recv()
@@ -374,31 +395,30 @@
         row = row + jnp.sum(d_ref[:, columns(mine, h)].astype(f32) * mm(low, every[1, :, at]), axis=0, keepdims=True)
         put_row(me, h, row)
         send_x(p).wait_recv()
-        hold[...] = big + xrx[p].astype(f32)
-        for way, behind in ((0, z), (1, outer - 1 - z)):
-            @pl.when(behind > 0)
-            def _():
-                send_z(way, p).wait_recv()
-                hold[...] = hold[...] + zrx[way, p].astype(f32)
-
-        p = me * halves + h
-        arx[p] = hold[...].astype(bf)
-        for way, behind in ((0, outer - 1 - z), (1, z)):
-            @pl.when(behind > 0)
-            def _():
-                give_z(way, p).start()
-
-        give_x(p).start()
-
-    def add_row(k, acc):
-        src = (me + k) % groups
-        send_row(me, src).wait_recv()
-        return acc + grx[src]
-
-    garx[me] = lax.fori_loop(1, groups, add_row, gtx[me])
+        big = big + xrx[p].astype(f32)
+
+        def add_end(k, acc):
+            src = across(k, z % 2)
+            send_end(z, h, src).wait_recv()
+            return acc + zend[src * halves + h].astype(f32)
+
+        big = lax.fori_loop(0, pairs - 1, add_end, big)
+        send_end(z, h, twin).wait_recv()
+        arx[me * halves + h] = (big + zend[twin * halves + h].astype(f32)).astype(bf)
+
+        def give(k, carry):
+            give_z(across(k, z % 2), z, h).start()
+            return carry
+
+        lax.fori_loop(0, pairs - 1, give, 0)
+        give_z(twin, z, h).start()
+        give_x(z, x, h).start()
+
+    batch(grx, groups - 1, sg, rg).wait_recv()
+    garx[me] = lax.fori_loop(1, groups, lambda k, acc: acc + grx[(me + k) % groups], gtx[me])
 
     def spread_row(k, carry):
-        give_row((me + k) % groups, me).start()
+        give_row((me + k) % groups).start()
         return carry
 
     lax.fori_loop(1, groups, spread_row, 0)
@@ -411,24 +431,30 @@
         else:
             pl.when(c < chunks)(go)
 
-    def pass_on(k, carry):
-        q = far(outer - 2 - k)
-        c = q * inner + x
-        way = jnp.where(q < z, 0, 1)
-        ahead = jnp.where(q < z, outer - 1 - z, z)
+    def hand_over(q, h):
+        give_x(q, x, h).start()
+        write(q * inner + x, h)
+
+    for h in range(halves):
+        def from_across(k, carry):
+            q = across(k, z % 2)
+            give_z(z, q, h).wait_recv()
+            give_z(twin, q, h).start()
+            hand_over(q, h)
+            return carry
+
+        lax.fori_loop(0, pairs - 1, from_across, 0)
+        give_z(z, twin, h).wait_recv()
+        hand_over(twin, h)
+
+    def from_twin(k, carry):
+        q = across(k, twin % 2)
         for h in range(halves):
-            p = c * halves + h
-            give_z(way, p).wait_recv()
-
-            @pl.when(ahead > 0)
-            def _():
-                give_z(way, p).start()
-
-            give_x(p).start()
-            write(c, h)
-        return carry
-
-    lax.fori_loop(0, outer - 1, pass_on, 0)
+            give_z(z, q, h).wait_recv()
+            hand_over(q, h)
+        return carry
+
+    lax.fori_loop(0, pairs - 1, from_twin, 0)
     for h in range(halves):
         write(me, h)
 
@@ -437,72 +463,44 @@
             gout_ref[:, pl.ds(pl.multiple_of(c * part + 128 * i, 128), 128)] = garx[c, i:i + 1, :]
         return carry
 
-    def wait_row(k, carry):
-        give_row(me, (me + k) % groups).wait_recv()
-        return carry
-
-    lax.fori_loop(1, groups, wait_row, 0)
+    batch(garx, groups - 1, sga, rga).wait_recv()
     lax.fori_loop(0, chunks, write_row, 0)
 
-    def last(k, carry):
-        c = far(outer - 1 - k) * inner + 1 - x
+    def last(q, h):
+        give_x(q, 1 - x, h).wait_recv()
+        write(q * inner + 1 - x, h)
+
+    for h in range(halves):
+        last(z, h)
+    for h in range(halves):
+        def last_across(k, carry):
+            last(across(k, z % 2), h)
+            return carry
+
+        lax.fori_loop(0, pairs - 1, last_across, 0)
+        last(twin, h)
+
+    def last_twin(k, carry):
         for h in range(halves):
-            give_x(c * halves + h).wait_recv()
-            write(c, h)
-        return carry
-
-    lax.fori_loop(0, outer, last, 0)
-
-    for w in range(2):
-        for k in range(step, total, step):
-            weights(w, (my + k) % total, my).wait_send()
-            if step == 2:
-                share(w, (my + k) % total).wait_send()
-        if step == 2:
-            weights(w, mate, my).wait_send()
-    for k in range(1, total):
-        j = (my + k) % total
-        owns(j, my).wait_send()
-        all_grams(j, my).wait_send()
+            last(across(k, twin % 2), h)
+        return carry
+
+    lax.fori_loop(0, pairs - 1, last_twin, 0)
+
+    sent = every.at[:, pl.ds(0, (total - 1) * rank), :]
+    remote(sent, sent, s1, rm.at[0], section=my).wait_send()
+    all_of_owns.wait_send()
+    all_of_tables.wait_send()
+    all_of_grams.wait_send()
     mix_x().wait_send()
     mix_back(x).wait_send()
-    for h in range(halves):
-        p = me * halves + h
-        for way, behind in ((0, outer - 1 - z), (1, z)):
-            @pl.when(behind > 0)
-            def _():
-                give_z(way, p).wait_send()
-
-    def left_dp(k, carry):
-        j = (me + k) % groups
-        grams(j, me).wait_send()
-        send_row(j, me).wait_send()
-        give_row(j, me).wait_send()
-        return carry
-
-    lax.fori_loop(1, groups, left_dp, 0)
-
-    def left_z(k, carry):
-        q = (z + k) % outer
-        mix_z(q, z).wait_send()
-        ahead = jnp.where(q < z, outer - 1 - z, z)
-        for h in range(halves):
-            send_z(jnp.where(q > z, 0, 1), q * halves + h).wait_send()
-
-            @pl.when(ahead > 0)
-            def _():
-                give_z(jnp.where(q < z, 0, 1), (q * inner + x) * halves + h).wait_send()
-        return carry
-
-    lax.fori_loop(1, outer, left_z, 0)
-
-    def left_x(q, carry):
-        for h in range(halves):
-            send_x(q * halves + h).wait_send()
-            give_x((q * inner + x) * halves + h).wait_send()
-        return carry
-
-    lax.fori_loop(0, outer, left_x, 0)
+    batch(mix_zrx, outer - 1, smz, rmz).wait_send()
+    batch(gtx, groups - 1, sg, rg).wait_send()
+    batch(garx, groups - 1, sga, rga).wait_send()
+    batch(tx, outer * halves, sx, rx.at[0]).wait_send()
+    batch(ztx, (outer - 1) * halves, sz, rz.at[0]).wait_send()
+    batch(arx, outer * halves, sax, rax.at[0]).wait_send()
+    batch(arx, (outer - 1) * halves, saz, raz.at[0]).wait_send()
 
 
 def body(entry, gain, down, up, gout, lengths, keep):
@@ -536,17 +534,14 @@
         vm(2, total * rank, part),
         vm(total, 3 * rank + 16, rows, t=f32),
         vm(rank, total * rank), vm(groups, rank, total * rank), vm(total * rank, total * rank),
-        vm(pieces, rank, sub), vm(pieces, rank, sub), vm(pieces, rank, sub), vm(2, pieces, rank, sub),
-        vm(rank, sub, t=f32),
+        *[vm(pieces, rank, sub)] * 5,
         vm(groups, tall, 128, t=f32), vm(groups, tall, 128, t=f32), vm(groups, tall, 128, t=f32),
         vm(2, rank, total * rank), vm(rank, total * rank), vm(rank, total * rank),
         vm(outer, rank, total * rank), vm(2, rank, total * rank),
         vm(groups * halves, rank, sub),
-        dma(8), dma(2, total), dma(2, total), dma(2, total), dma(total), dma(total), dma(groups), dma(groups),
-        dma(total), dma(total),
-        dma(pieces), dma(pieces), dma(pieces), dma(2, pieces), dma(groups), dma(groups), dma(groups), dma(groups),
-        one, one, dma(outer), dma(outer), one, one,
-        dma(2, groups * halves), dma(groups * halves), dma(groups * halves), dma(groups * halves),
+        dma(8), one, dma(2, -(-total // 2) if total % 2 == 0 else total), dma(2), *[one] * 6,
+        one, dma(pieces), one, dma(pieces), dma(pieces), *[one] * 4,
+        *[one] * 6, one, dma(pieces), one, dma(pieces),
     ]
     inside = pl.BlockSpec(memory_space=pltpu.VMEM)
     outside = pl.BlockSpec(memory_space=pltpu.HBM)

time: 54.6 us -> 50.1 us (0.918)
  Pallas kernels: 51.9 us -> 47.5 us
    pallas_call x1, Pallas kernels: 51.9 us -> 47.5 us  [body(): pl.pallas_call(functools.partial(kernel, sizes), out_shape=(jax.ShapeDtyp...]
where the time goes in v4:
time: 50.1 us; the launch traced here: 50 us
  Pallas kernels  47.5 us (95%)
  other arithmetic  1.25 us (2%)
  between operations  0.64 us (1%)
  local copies, waits for them, and re-layouts  0.61 us (1%)
    pallas_call x1, Pallas kernels, body(): pl.pallas_call(functools.partial(kernel, sizes), out_shape=(jax.ShapeDtyp...  47.5 us
    convert_element_type x1, other arithmetic, body(): return (up_grad[None, :, :width].astype(f32), gain_grad[:, :width])  1.25 us

profile of v4, /device:TPU:0, one launch (start us, length us, event | category | flops | bytes accessed | tf_op | source)
XLA Modules:
  0.0 50.0 jit_solution(6408012261725413189)
XLA Ops:
  0.6 47.5 %relay.1 = (bf16[48,8192]{1,0:T(8,128)(2,1)S(1)}, f32[1,8192]{1,0:T(1,128)S(1)}) custom-call(s32[1,8]{1,0:T(1,128)} %len_hbm.1, s32[8,16]{1,0:T(8,128)} %bitcast.12, bf16[1,8192]{1,0:T(2,128)(2,1)} %gain_hbm.1, bf16[128,8192]{1,0:T(8,128)(2,1)} %bitcast.8, bf16[128,8192]{1,0:T(8,128)(2,1)} %bitcast.9, bf16[48,8192]{1,0:T(8,128)(2,1)} %bitcast.10, ...), custom_call_target="tpu_custom_call" | custom-call | tf_op jit(solution)/shard_map/relay/pallas_call | solution.py:548
  48.1 1.2 %bitcast_convert_fusion = f32[1,48,8192]{2,1,0:T(8,128)} fusion(bf16[48,8192]{1,0:T(8,128)(2,1)S(1)} %get-tuple-element.4), kind=kLoop, calls=%fused_computation | loop fusion | flops 393216 | bytes 2359296 | tf_op jit(solution)/shard_map/convert_element_type | solution.py:558
  49.4 0.6 %copy.10 = f32[1,8192]{1,0:T(1,128)} copy(f32[1,8192]{1,0:T(1,128)S(1)} %get-tuple-element.9) | data formatting | bytes 65536
